TPU v7x, 32 devices: a whole 2x2x4 slice. The times are simulated.
32 devices in a mesh: dp: 4 (over x, y), sp: 8 (over z, core).
Axes of the slice: x: 2, y: 2, z: 4, core: 2. Of those that a mesh axis runs over, the one named last changes fastest.
Arguments:
- q: bfloat16 [128, 96, 128], P('dp'), parts along dimension 0
- k: bfloat16 [128, 8192, 8, 128], P('dp', 'sp'), parts along dimension 0
- v: bfloat16 [128, 8192, 8, 128], P('dp', 'sp'), parts along dimension 0
Outputs:
- q: bfloat16 [128, 96, 128], P('dp'), parts along dimension 0
There are 4 independent parts. A program takes and returns all parts, laid end to end along the dimension named above; each array names one.
All inputs are finite; a program needn't handle non-finite values.
Results may differ from a plain program's by a relative error of at most 0.012.
Values are sent between devices in bfloat16 or wider.
A program may use at most 2 GiB of HBM per device.

v0:
```python
import jax
import jax.numpy as jnp
from jax import lax
from jax.sharding import PartitionSpec as P


def einsum(form, a, b):
    return jnp.einsum(form, a.astype(jnp.float32), b.astype(jnp.float32))


def part_of(q, k, v):
    grouped = q.reshape(q.shape[0], k.shape[2], -1, q.shape[2])
    scores = einsum("bgsd,bugd->bgsu", grouped, k) * q.shape[2] ** -0.5
    high = jnp.max(scores, -1, keepdims=True)
    weights = jnp.exp(scores - high)
    seen = einsum("bgsu,bugd->bgsd", weights.astype(jnp.bfloat16), v)
    return jnp.concatenate([seen, jnp.sum(weights, -1, keepdims=True), high], -1)


def together(parts):
    seen, total, high = parts[..., :-2], parts[..., -2:-1], parts[..., -1:]
    scale = jnp.exp(high - jnp.max(high, 0))
    return (jnp.sum(seen * scale, 0) / jnp.sum(total * scale, 0)).astype(jnp.bfloat16)


def solution(mesh):
    def step(q, k, v):
        return together(lax.all_gather(part_of(q, k, v), "sp")).reshape(q.shape)

    return jax.shard_map(
        step,
        mesh=mesh,
        in_specs=(P("dp", None, None), P("dp", "sp", None, None), P("dp", "sp", None, None)),
        out_specs=P("dp", None, None),
        check_vma=False,
    )
```

profile of v0, /device:TPU:0, one launch (start us, length us, event | category | flops | bytes accessed | tf_op | source)
XLA Modules:
  0.0 373.1 jit_solution(9512018866424847679)
XLA Ops:
  6.5 0.0 all-gather.3.cloned.1.call-start
  6.5 1.4 copy.46
  8.0 31.9 %multiply_reduce_fusion = (f32[32,8,12]{2,1,0:T(8,128)S(1)}, f32[32,8,12,1024]{3,2,1,0:T(8,128)}) fusion(bf16[32,1024,8,128]{3,2,1,0:T(8,128)(2,1)} %param.4, bf16[32,8,12,128]{3,0,2,1:T(8,128)(2,1)S(1)} %bitcast.14), kind=kOutput, calls=%fused_computation.5 | convolution fusion | flops 811594752 | bytes 80490496 | tf_op jit(solution)/shard_map/bgsd,bugd->bgsu/dot_general | solution.py:8
  39.9 7.8 %fusion.4 = f32[32,8,12]{2,1,0:T(8,128)S(1)} fusion(f32[32,8,12,1024]{3,2,1,0:T(8,128)} %get-tuple-element.11, f32[32,8,12]{2,1,0:T(8,128)S(1)} %get-tuple-element.10), kind=kLoop, calls=%fused_computation.6 | loop fusion | flops 9434112 | bytes 12607488 | tf_op jit(solution)/shard_map/reduce_sum | solution.py:17
  47.7 31.1 %fusion = f32[32,8,12,128]{3,2,1,0:T(8,128)} fusion(bf16[32,1024,8,128]{3,2,1,0:T(8,128)(2,1)} %param.5, f32[32,8,12,1024]{3,2,1,0:T(8,128)} %get-tuple-element.11, f32[32,8,12]{2,1,0:T(8,128)S(1)} %get-tuple-element.10), kind=kOutput, calls=%fused_computation | convolution fusion | flops 814743552 | bytes 81276928 | tf_op jit(solution)/shard_map/bgsu,bugd->bgsd/dot_general | solution.py:8
  78.8 1.7 copy.52
  80.5 3.0 copy.53
  83.5 3.0 pad_maximum_fusion
  86.5 4.6 %copy.54 = f32[32,8,12,130]{3,1,2,0:T(8,128)} copy(f32[32,8,12,130]{3,2,1,0:T(8,128)S(1)} %pad_maximum_fusion) | data formatting | bytes 3194880 | tf_op jit(solution)/shard_map/concatenate | solution.py:17
  91.1 0.0 all-gather.3.cloned.1.call-update
  91.2 223.2 %all-gather.3.cloned.1.call-done = f32[256,8,12,130]{3,1,2,0:T(8,128)} async-done(((f32[32,8,12,130]{3,1,2,0:T(8,128)}), f32[256,8,12,130]{3,1,2,0:T(8,128)}) %all-gather.3.cloned.1.call-update) | async-done | bytes 12779536 | tf_op jit(solution)/shard_map/all_gather | solution.py:28
  314.4 22.0 %fusion.14 = (f32[8,32,8,12,1]{4,2,3,1,0:T(8,128)}, f32[32,8,12]{1,2,0:T(8,128)S(1)}, f32[8,32,8,12,1]{4,2,3,1,0:T(8,128)}) fusion(f32[8,32,8,12,130]{4,2,3,1,0:T(8,128)} %bitcast.12), kind=kLoop, calls=%fused_computation.21 | loop fusion | flops 21504 | bytes 405504 | tf_op jit(solution)/shard_map/slice | solution.py:21
  336.4 9.1 %copy.68 = f32[8,32,8,12,1]{1,2,4,3,0:T(8,128)S(1)} copy(f32[8,32,8,12,1]{4,2,3,1,0:T(8,128)} %get-tuple-element.5) | data formatting | bytes 196608
  345.5 0.1 copy.70
  345.7 9.1 %copy.67 = f32[8,32,8,12,1]{1,2,4,3,0:T(8,128)S(1)} copy(f32[8,32,8,12,1]{4,2,3,1,0:T(8,128)} %get-tuple-element.7) | data formatting | bytes 196608
  354.8 0.1 multiply_reduce_fusion.1
  354.9 0.9 copy.56
  355.8 7.8 %fusion.6 = f32[32,8,12,128]{3,1,2,0:T(8,128)S(1)} fusion(f32[8,32,8,12,130]{4,2,3,1,0:T(8,128)} %bitcast.13, f32[8,32,8,12]{2,3,1,0:T(8,128)S(1)} %copy.56), kind=kLoop, calls=%fused_computation.9 | loop fusion | flops 5898240 | bytes 14254080 | tf_op jit(solution)/shard_map/reduce_sum | solution.py:23
  363.6 0.9 copy.58
  364.5 0.5 fusion.10
  365.0 1.2 copy.61
  (2 shorter events, 0.0 us)
Async XLA Ops:
  6.5 307.9 %all-gather.3.cloned.1.call-start = ((), (), s32[]{:S(2)}) async-start(), calls=%async_computation | async-start | bytes 28311552 | tf_op jit(solution)/shard_map/all_gather | solution.py:28
Sparse Core Ops, SparseCore 0:
  91.3 223.0 all-gather.2
where the time goes:
time: 374 us; the launch traced here: 373 us
  waiting for transfers between devices  223 us (60%)
  matrix products  63 us (17%)
  other arithmetic  41.3 us (11%)
  local copies, waits for them, and re-layouts  32.1 us (9%)
  between operations  13.5 us (4%)
    all_gather x1, waiting for transfers between devices, step(): return together(lax.all_gather(part_of(q, k, v), 'sp')).reshape(q.shape)  223 us
    dot_general x2, matrix products, einsum(): return jnp.einsum(form, a.astype(jnp.float32), b.astype(jnp.float32))  63 us
    slice x1, other arithmetic, together(): seen, total, high = (parts[..., :-2], parts[..., -2:-1], parts[..., -1:])  22 us
    unnamed x4, local copies, waits for them, and re-layouts  19.8 us
    reduce_sum x1, other arithmetic, together(): jnp.sum(seen * scale, 0) / jnp.sum(total * scale, 0)  7.82 us
    reduce_sum x1, other arithmetic, part_of(): jnp.sum(weights, -1, keepdims=True)  7.81 us
  transfers between devices with their start and end apart: 1, of which 1 were waited for; matrix products, arithmetic and copies ran while one was open for 0% of the time, Pallas kernels for 0%

commit v1 on v0

v1 whole, which is shorter than its diff:
```python
import functools

import jax
import jax.numpy as jnp
from jax import lax
from jax.experimental import pallas as pl
from jax.experimental.pallas import tpu as pltpu
from jax.sharding import PartitionSpec as P

F32, BF16 = jnp.float32, jnp.bfloat16
LOG2E = 1.4426950408889634
GROUP = 16
STEP = 4
CHUNK = 512


def place(rows, cols, wide, given):
    r = lax.broadcasted_iota(jnp.int32, (rows, cols), 0)
    c = lax.broadcasted_iota(jnp.int32, (rows, cols), 1)
    return jnp.where((r % wide < given) & (c == r // wide * given + r % wide), 1.0, 0.0).astype(BF16)


def take(rows, cols, wide, given):
    r = lax.broadcasted_iota(jnp.int32, (rows, cols), 0)
    c = lax.broadcasted_iota(jnp.int32, (rows, cols), 1)
    return jnp.where((c % wide < given) & (r == c // wide * given + c % wide), 1.0, 0.0).astype(BF16)


def classes(x, heads, f):
    step = heads
    while step < 128:
        x = f(x, pltpu.roll(x, step, 1))
        step *= 2
    return x


def kernel(n, heads, devices, q_ref, k_hbm, v_hbm, out, *scratch):
    kb, vb = scratch[:STEP], scratch[STEP : 2 * STEP]
    (qq, r_ref, mx, pm, pmt, px, pxt, obuf, sbuf, orecv, srecv, fbuf) = scratch[2 * STEP : 2 * STEP + 12]
    (ksem, vsem, o_send, s_send, o_recv, s_recv, f_send, f_recv, f_own) = scratch[2 * STEP + 12 :]
    rows = k_hbm.shape[1]
    half = rows // 2
    total = heads * GROUP
    given = q_ref.shape[1] // heads
    part = q_ref.shape[1] // 2
    scale = q_ref.shape[2] ** -0.5 * LOG2E
    steps = n // STEP
    me = lax.axis_index("sp")
    chip, core = me // 2, me % 2
    mine = (chip + STEP - 1) % STEP

    lane = lax.broadcasted_iota(jnp.int32, (GROUP, 128), 1)
    masks = [lane % heads == h for h in range(heads)]
    keep = [m.astype(F32).astype(BF16) for m in masks]
    lane8 = lane[:8]

    def kcopy(u, i):
        return pltpu.make_async_copy(k_hbm.at[jnp.minimum(i * STEP + u, n - 1)], kb[u].at[i % 2], ksem.at[u, i % 2])

    def vcopy(u, i):
        return pltpu.make_async_copy(v_hbm.at[jnp.minimum(i * STEP + u, n - 1)], vb[u].at[i % 2], vsem.at[u, i % 2])

    def o_copy(b, d):
        peer = (me + d) % devices
        turn = (peer // 2 + STEP - 1) % STEP
        return pltpu.make_async_remote_copy(
            obuf.at[b, turn, peer % 2], orecv.at[b + 2, d], o_send.at[b, d], o_recv.at[b, d], device_id={"sp": peer}
        )

    def s_copy(b, d):
        peer = (me + d) % devices
        turn = (peer // 2 + STEP - 1) % STEP
        return pltpu.make_async_remote_copy(
            sbuf.at[b, turn], srecv.at[b + 2, d], s_send.at[b, d], s_recv.at[b, d], device_id={"sp": peer}
        )

    def f_copy(b, d):
        peer = (me + d) % devices
        return pltpu.make_async_remote_copy(
            fbuf.at[b + 2], out.at[jnp.minimum(b * STEP + mine, n), core], f_send.at[b, d], f_recv.at[b, d], device_id={"sp": peer}
        )

    def f_local(b):
        return pltpu.make_async_copy(fbuf.at[b + 2], out.at[jnp.minimum(b * STEP + mine, n), core], f_own.at[b])

    others = range(1, devices)

    def send_parts(b):
        for d in others:
            o_copy(b, d).start()
            s_copy(b, d).start()

    def wait_parts(b):
        for d in others:
            o_copy(b, d).wait_recv()
            s_copy(b, d).wait_recv()

    def sent_parts(b):
        for d in others:
            o_copy(b, d).wait_send()
            s_copy(b, d).wait_send()

    def send_result(b):
        f_local(b).start()
        for d in others:
            f_copy(b, d).start()

    def done_result(b):
        f_local(b).wait()
        for d in others:
            f_copy(b, d).wait_send()
            f_copy(b, d).wait_recv()

    def combine(b):
        own = jnp.maximum(b, 0)
        stats = [sbuf[own, mine]] + [srecv[b + 2, d] for d in others]
        parts = [obuf[own, mine, core]] + [orecv[b + 2, d] for d in others]
        high = functools.reduce(jnp.maximum, stats)
        scales = [jnp.exp2((s - high) * scale) for s in stats]
        below = functools.reduce(jnp.add, [a * pltpu.roll(s, 128 - heads, 1) for a, s in zip(scales, stats)])
        inverse = 1.0 / below
        wide = jnp.dot(px[...], jnp.concatenate(parts, 1), preferred_element_type=F32)
        sums = jnp.zeros((total // 2, 128), F32)
        for d, a in enumerate(scales):
            w = a * inverse
            w = jnp.where(core == 0, w, pltpu.roll(w, 128 - heads // 2, 1))
            spread = jnp.concatenate(
                [
                    jnp.broadcast_to(w[:, 64 * (e % 2) + e // 2 : 64 * (e % 2) + e // 2 + 1], (8, 128))
                    for e in range(heads)
                ],
                0,
            )
            sums = sums + wide[:, d * 128 : (d + 1) * 128] * spread
        fbuf[b + 2] = jnp.dot(pxt[...], sums.astype(BF16), preferred_element_type=F32).astype(BF16)

    def values(high, source, v, b, u):
        base = high * scale
        seen = jnp.zeros((2 * total, 256), F32)
        sums = jnp.zeros((GROUP, 128), F32)
        t = CHUNK // 128 if half >= CHUNK else half // 128
        size = t * 128
        for c in range(half // size):
            parts = []
            for side in range(2):
                for x in range(t):
                    p = jnp.exp2(r_ref[source, side, :, pl.ds(c * size + x * 128, 128)] * scale - base)
                    sums = sums + p
                    parts.append(p.astype(BF16))
            spread = jnp.concatenate(
                [
                    jnp.concatenate([parts[side * t + x] * keep[h] for x in range(t)], 1)
                    for side in range(2)
                    for h in range(heads)
                ],
                0,
            )
            vv = jnp.concatenate([v[pl.ds(c * size, size)], v[pl.ds(half + c * size, size)]], 1)
            seen = seen + jnp.dot(spread, vv, preferred_element_type=F32)
            yield
        sums = classes(sums, heads, jnp.add)
        o = (seen[:total, :128] + seen[total:, 128:]).astype(BF16)
        o = jnp.dot(pmt[...], o, preferred_element_type=F32).astype(BF16)
        obuf[b, u, 0] = o[:part]
        obuf[b, u, 1] = o[part:]
        first = lane8 // heads % 2 == 0
        low = jnp.where(first, high[:8], sums[:8])
        high = jnp.where(first, high[8:], sums[8:])
        sbuf[b, u] = jnp.where(lane8 < 64, low, high)
        yield

    def scores(query, target, k, best):
        t = CHUNK // 128 if half >= CHUNK else half // 128
        size = t * 128
        for c in range(half // size):
            kk = jnp.concatenate([k[pl.ds(c * size, size)], k[pl.ds(half + c * size, size)]], 1)
            s = lax.dot_general(query, kk, (((1,), (1,)), ((), ())), preferred_element_type=F32)
            for side in range(2):
                for x in range(t):
                    cols = slice(x * 128, (x + 1) * 128)
                    r = s[side * total : side * total + GROUP, cols]
                    for h in range(1, heads):
                        first = side * total + h * GROUP
                        r = jnp.where(masks[h], s[first : first + GROUP, cols], r)
                    r_ref[target, side, :, pl.ds(c * size + x * 128, 128)] = r
                    best[0] = jnp.maximum(best[0], r)
            yield

    for i in range(2):
        for u in range(STEP):
            kcopy(u, i).start()
            if (i, u) != (1, STEP - 1):
                vcopy(u, i).start()

    barrier = pltpu.get_barrier_semaphore()
    for d in others:
        pl.semaphore_signal(barrier, inc=1, device_id={"sp": (me + d) % devices})
    pl.semaphore_wait(barrier, devices - 1)

    pm[...] = place(total, q_ref.shape[1], GROUP, given)
    pmt[...] = take(q_ref.shape[1], total, GROUP, given)
    px[...] = place(total // 2, part, GROUP, given)
    pxt[...] = take(part, total // 2, GROUP, given)
    qq[...] = jnp.zeros_like(qq)
    r_ref[...] = jnp.zeros_like(r_ref)
    mx[...] = jnp.zeros_like(mx)

    def step(i, _):
        @pl.when(i >= 1)
        def _():
            send_parts(i - 1)
            vcopy(STEP - 1, i - 1).wait()

        @pl.when(i >= 3)
        def _():
            send_result(i - 3)

        @pl.when(i >= 2)
        def _():
            wait_parts(i - 2)
            sent_parts(i - 2)

        @pl.when(i >= 5)
        def _():
            done_result(i - 5)

        for u in range(STEP):
            kcopy(u, i).wait()
            if u < STEP - 1:
                vcopy(u, i).wait()

        combine(i - 2)
        for u in range(STEP):
            qp = jnp.dot(pm[...], q_ref[i * STEP + u], preferred_element_type=F32).astype(BF16)
            qq[u, :total, :128] = qp
            qq[u, total:, 128:] = qp
        best = [mx[...]]
        for u in range(STEP):
            high = classes(best[0], heads, jnp.maximum)
            best = [jnp.full((GROUP, 128), -jnp.inf, F32)]
            w = (u + STEP - 1) % STEP
            a = values(high, (u + STEP - 1) % 2, vb[w].at[i % 2 if u else (i + 1) % 2], i, u)
            b = scores(qq[u], u % 2, kb[u].at[i % 2], best)
            for _ in b:
                next(a)
            next(a)

            @pl.when(i < steps - 2)
            def _():
                kcopy(u, i + 2).start()

            @pl.when(i < (steps - 2 if u else steps - 1))
            def _():
                vcopy(w, i + 2 if u else i + 1).start()

        mx[...] = best[0]
        return 0

    lax.fori_loop(0, steps, step, 0)

    send_parts(steps - 1)
    send_result(steps - 3)
    wait_parts(steps - 2)
    vcopy(STEP - 1, steps - 1).wait()
    combine(steps - 2)
    for _ in values(
        classes(mx[...], heads, jnp.maximum), (STEP - 1) % 2, vb[STEP - 1].at[(steps - 1) % 2], steps, 0
    ):
        pass
    send_result(steps - 2)

    b = steps
    for c in range(2):
        d = (2 + c - me + devices) % devices

        @pl.when(d != 0)
        def _():
            o_copy(b, d).start()
            s_copy(b, d).start()

    wait_parts(steps - 1)
    combine(steps - 1)
    send_result(steps - 1)

    @pl.when(chip == 1)
    def _():
        wait_parts(b)
        combine(b)
        send_result(b)

    sent_parts(steps - 2)
    sent_parts(steps - 1)
    for c in range(2):
        d = (2 + c - me + devices) % devices

        @pl.when(d != 0)
        def _():
            o_copy(b, d).wait_send()
            s_copy(b, d).wait_send()

    for i in range(max(steps - 5, 0), steps):
        done_result(i)

    @pl.when(chip == 1)
    def _():
        f_local(b).wait()
        for d in others:
            f_copy(b, d).wait_send()

    for c in range(2):
        d = (me - 2 - c + devices) % devices

        @pl.when(d != 0)
        def _():
            f_copy(b, d).wait_recv()


def solution(mesh):
    devices = mesh.shape["sp"]

    def step(q, k, v):
        n, tokens, heads, d = k.shape
        rows, queries = tokens * heads, q.shape[1]
        total, part, batches = heads * GROUP, queries // 2, n // STEP + 1
        dma = pltpu.SemaphoreType.DMA
        out = pl.pallas_call(
            functools.partial(kernel, n, heads, devices),
            in_specs=[pl.BlockSpec(memory_space=pltpu.VMEM)] + [pl.BlockSpec(memory_space=pl.ANY)] * 2,
            out_specs=pl.BlockSpec(memory_space=pl.ANY),
            out_shape=jax.ShapeDtypeStruct((batches * STEP - STEP + 1, 2, part, d), BF16),
            scratch_shapes=[pltpu.VMEM((2, rows, d), BF16)] * (2 * STEP)
            + [
                pltpu.VMEM((STEP, 2 * total, 2 * d), BF16),
                pltpu.VMEM((2, 2, GROUP, rows // 2), F32),
                pltpu.VMEM((GROUP, 128), F32),
                pltpu.VMEM((total, queries), BF16),
                pltpu.VMEM((queries, total), BF16),
                pltpu.VMEM((total // 2, part), BF16),
                pltpu.VMEM((part, total // 2), BF16),
                pltpu.VMEM((batches, STEP, 2, part, d), BF16),
                pltpu.VMEM((batches, STEP, 8, 128), F32),
                pltpu.VMEM((batches + 2, devices, part, d), BF16),
                pltpu.VMEM((batches + 2, devices, 8, 128), F32),
                pltpu.VMEM((batches + 2, part, d), BF16),
                dma((STEP, 2)),
                dma((STEP, 2)),
                dma((batches, devices)),
                dma((batches, devices)),
                dma((batches, devices)),
                dma((batches, devices)),
                dma((batches, devices)),
                dma((batches, devices)),
                dma((batches,)),
            ],
            compiler_params=pltpu.CompilerParams(
                collective_id=0, has_side_effects=True, vmem_limit_bytes=62 << 20
            ),
            name="attend",
        )(q, k.reshape(n, rows, d), v.reshape(n, rows, d))
        return out[1:].reshape(q.shape)

    return jax.shard_map(
        step,
        mesh=mesh,
        in_specs=(P("dp", None, None), P("dp", "sp", None, None), P("dp", "sp", None, None)),
        out_specs=P("dp", None, None),
        check_vma=False,
    )
```

time: 374 us -> 82.8 us (0.22)
  waiting for transfers between devices: 223 us -> 0 us
  Pallas kernels: 0 us -> 80.5 us
  matrix products: 63 us -> 0 us
  other arithmetic: 41.3 us -> 0 us
  local copies, waits for them, and re-layouts: 32.1 us -> 2.06 us
  between operations: 13.5 us -> 0.01 us
    all_gather x1 -> x0, waiting for transfers between devices: 223 us -> none  [step(): return together(lax.all_gather(part_of(q, k, v), 'sp')).reshape(q.shape)]
    pallas_call x0 -> x1, Pallas kernels: none -> 80.5 us  [step(): pl.pallas_call(functools.partial(kernel, n, heads, devices), in_specs=[pl...]
    dot_general x2 -> x0, matrix products: 63 us -> none  [einsum(): return jnp.einsum(form, a.astype(jnp.float32), b.astype(jnp.float32))]
    slice x1 -> x0, other arithmetic: 22 us -> none  [together(): seen, total, high = (parts[..., :-2], parts[..., -2:-1], parts[..., -1:])]
    unnamed x4 -> x0, local copies, waits for them, and re-layouts: 19.8 us -> none
    reduce_sum x3 -> x0, other arithmetic: 15.7 us -> none  [the longest x1 7.82 us: together(): jnp.sum(seen * scale, 0) / jnp.sum(total * scale, 0)]
    broadcast_in_dim x2 -> x0, local copies, waits for them, and re-layouts: 4.67 us -> none  [the longest x1 3.01 us: part_of(): high = jnp.max(scores, -1, keepdims=True)]
    concatenate x1 -> x0, local copies, waits for them, and re-layouts: 4.61 us -> none  [part_of(): jnp.concatenate([seen, jnp.sum(weights, -1, keepdims=True), high], -1)]
  transfers between devices with their start and end apart: 1 -> 0, of which waited for: 1 -> 0; matrix products, arithmetic and copies ran while one was open for 0% -> 0% of each run, Pallas kernels for 0% -> 0%
where the time goes in v1:
time: 82.8 us; the launch traced here: 82.6 us
  Pallas kernels  80.5 us (97%)
  local copies, waits for them, and re-layouts  2.06 us (2%)
    pallas_call x1, Pallas kernels, step(): pl.pallas_call(functools.partial(kernel, n, heads, devices), in_specs=[pl...  80.5 us
    slice x1, local copies, waits for them, and re-layouts, step(): return out[1:].reshape(q.shape)  2.06 us

profile of v1, /device:TPU:0, one launch (start us, length us, event | category | flops | bytes accessed | tf_op | source)
XLA Modules:
  0.0 82.6 jit_solution(1923432968913619233)
XLA Ops:
  0.0 80.5 %attend.1 = bf16[33,2,48,128]{3,2,1,0:T(8,128)(2,1)} custom-call(bf16[32,96,128]{2,1,0:T(8,128)(2,1)} %q_ref.1, bf16[32,8192,128]{2,1,0:T(8,128)(2,1)} %bitcast.k_hbm, bf16[32,8192,128]{2,1,0:T(8,128)(2,1)} %bitcast.1.v_hbm), custom_call_target="tpu_custom_call" | custom-call | tf_op jit(solution)/shard_map/attend/pallas_call | solution.py:326
  80.6 2.1 %slice.3 = bf16[32,2,48,128]{3,2,1,0:T(8,128)(2,1)} slice(bf16[33,2,48,128]{3,2,1,0:T(8,128)(2,1)} %attend.1), slice={[1:33], [0:2], [0:48], [0:128]} | slice | bytes 1572864 | tf_op jit(solution)/shard_map/slice | solution.py:360

commit v2 on v1

--- a/solution.py
+++ b/solution.py
@@ -14,16 +14,17 @@
 CHUNK = 512
 
 
-def place(rows, cols, wide, given):
-    r = lax.broadcasted_iota(jnp.int32, (rows, cols), 0)
-    c = lax.broadcasted_iota(jnp.int32, (rows, cols), 1)
-    return jnp.where((r % wide < given) & (c == r // wide * given + r % wide), 1.0, 0.0).astype(BF16)
-
-
-def take(rows, cols, wide, given):
-    r = lax.broadcasted_iota(jnp.int32, (rows, cols), 0)
-    c = lax.broadcasted_iota(jnp.int32, (rows, cols), 1)
-    return jnp.where((c % wide < given) & (r == c // wide * given + c % wide), 1.0, 0.0).astype(BF16)
+def packed(r, heads, given):
+    h, j = r // given, r % given
+    return jnp.where(j < 8, 8 * h + j, 8 * heads + (given - 8) * h + j - 8)
+
+
+def place(heads, given, back=False):
+    rows = heads * given
+    r = lax.broadcasted_iota(jnp.int32, (rows, rows), 0)
+    c = lax.broadcasted_iota(jnp.int32, (rows, rows), 1)
+    r, c = (c, r) if back else (r, c)
+    return jnp.where(r == packed(c, heads, given), 1.0, 0.0).astype(BF16)
 
 
 def classes(x, heads, f):
@@ -36,12 +37,14 @@
 
 def kernel(n, heads, devices, q_ref, k_hbm, v_hbm, out, *scratch):
     kb, vb = scratch[:STEP], scratch[STEP : 2 * STEP]
-    (qq, r_ref, mx, pm, pmt, px, pxt, obuf, sbuf, orecv, srecv, fbuf) = scratch[2 * STEP : 2 * STEP + 12]
-    (ksem, vsem, o_send, s_send, o_recv, s_recv, f_send, f_recv, f_own) = scratch[2 * STEP + 12 :]
+    (qq, r_ref, mx, pm, pxt, obuf, sbuf, orecv, srecv, fbuf) = scratch[2 * STEP : 2 * STEP + 10]
+    (ksem, vsem, o_send, s_send, o_recv, s_recv, f_send, f_recv, f_own) = scratch[2 * STEP + 10 :]
     rows = k_hbm.shape[1]
     half = rows // 2
-    total = heads * GROUP
-    given = q_ref.shape[1] // heads
+    total = q_ref.shape[1]
+    given = total // heads
+    first = heads * 8
+    pairs = heads // 2
     part = q_ref.shape[1] // 2
     scale = q_ref.shape[2] ** -0.5 * LOG2E
     steps = n // STEP
@@ -50,9 +53,14 @@
     mine = (chip + STEP - 1) % STEP
 
     lane = lax.broadcasted_iota(jnp.int32, (GROUP, 128), 1)
-    masks = [lane % heads == h for h in range(heads)]
-    keep = [m.astype(F32).astype(BF16) for m in masks]
+    row = lax.broadcasted_iota(jnp.int32, (GROUP, 128), 0)
+    kind = lane % heads
     lane8 = lane[:8]
+    masks = [kind[:8] == h for h in range(heads)]
+    twos = [kind[:8] // 2 == p for p in range(pairs)]
+    keep = [kind == 2 * g + row // 8 for g in range(pairs)]
+    keep += [kind == 4 * g + row // 4 for g in range(pairs // 2)]
+    keep = [m.astype(F32).astype(BF16) for m in keep]
 
     def kcopy(u, i):
         return pltpu.make_async_copy(k_hbm.at[jnp.minimum(i * STEP + u, n - 1)], kb[u].at[i % 2], ksem.at[u, i % 2])
@@ -119,19 +127,13 @@
         scales = [jnp.exp2((s - high) * scale) for s in stats]
         below = functools.reduce(jnp.add, [a * pltpu.roll(s, 128 - heads, 1) for a, s in zip(scales, stats)])
         inverse = 1.0 / below
-        wide = jnp.dot(px[...], jnp.concatenate(parts, 1), preferred_element_type=F32)
-        sums = jnp.zeros((total // 2, 128), F32)
-        for d, a in enumerate(scales):
+        sums = jnp.zeros((part, 128), F32)
+        for x, a in zip(parts, scales):
             w = a * inverse
             w = jnp.where(core == 0, w, pltpu.roll(w, 128 - heads // 2, 1))
-            spread = jnp.concatenate(
-                [
-                    jnp.broadcast_to(w[:, 64 * (e % 2) + e // 2 : 64 * (e % 2) + e // 2 + 1], (8, 128))
-                    for e in range(heads)
-                ],
-                0,
-            )
-            sums = sums + wide[:, d * 128 : (d + 1) * 128] * spread
+            w = [jnp.broadcast_to(w[:, e : e + 1], (8, 128)) for e in (*range(pairs), *range(64, 64 + pairs))]
+            w = w[:pairs] + [jnp.where(row[:8] < 4, w[pairs + p], w[pairs + p + 1]) for p in range(0, pairs, 2)]
+            sums = sums + x.astype(F32) * jnp.concatenate(w, 0)
         fbuf[b + 2] = jnp.dot(pxt[...], sums.astype(BF16), preferred_element_type=F32).astype(BF16)
 
     def values(high, source, v, b, u):
@@ -146,12 +148,12 @@
                 for x in range(t):
                     p = jnp.exp2(r_ref[source, side, :, pl.ds(c * size + x * 128, 128)] * scale - base)
                     sums = sums + p
-                    parts.append(p.astype(BF16))
+                    parts.append([jnp.concatenate([y, y], 0).astype(BF16) for y in (p[:8], p[8:])])
             spread = jnp.concatenate(
                 [
-                    jnp.concatenate([parts[side * t + x] * keep[h] for x in range(t)], 1)
+                    jnp.concatenate([parts[side * t + x][g // pairs] * m for x in range(t)], 1)
                     for side in range(2)
-                    for h in range(heads)
+                    for g, m in enumerate(keep)
                 ],
                 0,
             )
@@ -160,12 +162,12 @@
             yield
         sums = classes(sums, heads, jnp.add)
         o = (seen[:total, :128] + seen[total:, 128:]).astype(BF16)
-        o = jnp.dot(pmt[...], o, preferred_element_type=F32).astype(BF16)
-        obuf[b, u, 0] = o[:part]
-        obuf[b, u, 1] = o[part:]
-        first = lane8 // heads % 2 == 0
-        low = jnp.where(first, high[:8], sums[:8])
-        high = jnp.where(first, high[8:], sums[8:])
+        for c in range(2):
+            obuf[b, u, c, : first // 2] = o[c * first // 2 : (c + 1) * first // 2]
+            obuf[b, u, c, first // 2 :] = o[first + c * (part - first // 2) : first + (c + 1) * (part - first // 2)]
+        even = lane8 // heads % 2 == 0
+        low = jnp.where(even, high[:8], sums[:8])
+        high = jnp.where(even, high[8:], sums[8:])
         sbuf[b, u] = jnp.where(lane8 < 64, low, high)
         yield
 
@@ -178,10 +180,13 @@
             for side in range(2):
                 for x in range(t):
                     cols = slice(x * 128, (x + 1) * 128)
-                    r = s[side * total : side * total + GROUP, cols]
+                    block = [s[side * total + e : side * total + e + 8, cols] for e in range(0, total, 8)]
+                    r = [block[0], block[heads]]
                     for h in range(1, heads):
-                        first = side * total + h * GROUP
-                        r = jnp.where(masks[h], s[first : first + GROUP, cols], r)
+                        r[0] = jnp.where(masks[h], block[h], r[0])
+                    for p in range(1, pairs):
+                        r[1] = jnp.where(twos[p], block[heads + p], r[1])
+                    r = jnp.concatenate(r, 0)
                     r_ref[target, side, :, pl.ds(c * size + x * 128, 128)] = r
                     best[0] = jnp.maximum(best[0], r)
             yield
@@ -197,37 +202,35 @@
         pl.semaphore_signal(barrier, inc=1, device_id={"sp": (me + d) % devices})
     pl.semaphore_wait(barrier, devices - 1)
 
-    pm[...] = place(total, q_ref.shape[1], GROUP, given)
-    pmt[...] = take(q_ref.shape[1], total, GROUP, given)
-    px[...] = place(total // 2, part, GROUP, given)
-    pxt[...] = take(part, total // 2, GROUP, given)
+    pm[...] = place(heads, given)
+    pxt[...] = place(heads // 2, given, back=True)
     qq[...] = jnp.zeros_like(qq)
     r_ref[...] = jnp.zeros_like(r_ref)
     mx[...] = jnp.zeros_like(mx)
 
     def step(i, _):
-        @pl.when(i >= 1)
-        def _():
-            send_parts(i - 1)
-            vcopy(STEP - 1, i - 1).wait()
-
-        @pl.when(i >= 3)
-        def _():
-            send_result(i - 3)
-
-        @pl.when(i >= 2)
-        def _():
-            wait_parts(i - 2)
-            sent_parts(i - 2)
-
-        @pl.when(i >= 5)
-        def _():
-            done_result(i - 5)
-
         for u in range(STEP):
             kcopy(u, i).wait()
             if u < STEP - 1:
                 vcopy(u, i).wait()
+
+        @pl.when(i >= 1)
+        def _():
+            vcopy(STEP - 1, i - 1).wait()
+            send_parts(i - 1)
+
+        @pl.when(i >= 3)
+        def _():
+            send_result(i - 3)
+
+        @pl.when(i >= 2)
+        def _():
+            wait_parts(i - 2)
+            sent_parts(i - 2)
+
+        @pl.when(i >= 5)
+        def _():
+            done_result(i - 5)
 
         combine(i - 2)
         for u in range(STEP):
@@ -321,7 +324,7 @@
     def step(q, k, v):
         n, tokens, heads, d = k.shape
         rows, queries = tokens * heads, q.shape[1]
-        total, part, batches = heads * GROUP, queries // 2, n // STEP + 1
+        part, batches = queries // 2, n // STEP + 1
         dma = pltpu.SemaphoreType.DMA
         out = pl.pallas_call(
             functools.partial(kernel, n, heads, devices),
@@ -330,13 +333,11 @@
             out_shape=jax.ShapeDtypeStruct((batches * STEP - STEP + 1, 2, part, d), BF16),
             scratch_shapes=[pltpu.VMEM((2, rows, d), BF16)] * (2 * STEP)
             + [
-                pltpu.VMEM((STEP, 2 * total, 2 * d), BF16),
+                pltpu.VMEM((STEP, 2 * queries, 2 * d), BF16),
                 pltpu.VMEM((2, 2, GROUP, rows // 2), F32),
                 pltpu.VMEM((GROUP, 128), F32),
-                pltpu.VMEM((total, queries), BF16),
-                pltpu.VMEM((queries, total), BF16),
-                pltpu.VMEM((total // 2, part), BF16),
-                pltpu.VMEM((part, total // 2), BF16),
+                pltpu.VMEM((queries, queries), BF16),
+                pltpu.VMEM((part, part), BF16),
                 pltpu.VMEM((batches, STEP, 2, part, d), BF16),
                 pltpu.VMEM((batches, STEP, 8, 128), F32),
                 pltpu.VMEM((batches + 2, devices, part, d), BF16),

time: 82.8 us -> 73.5 us (0.89)
  Pallas kernels: 80.5 us -> 71.2 us
    pallas_call x1, Pallas kernels: 80.5 us -> 71.2 us  [step(): pl.pallas_call(functools.partial(kernel, n, heads, devices), in_specs=[pl...]
where the time goes in v2:
time: 73.5 us; the launch traced here: 73.3 us
  Pallas kernels  71.2 us (97%)
  local copies, waits for them, and re-layouts  2.06 us (3%)
    pallas_call x1, Pallas kernels, step(): pl.pallas_call(functools.partial(kernel, n, heads, devices), in_specs=[pl...  71.2 us
    slice x1, local copies, waits for them, and re-layouts, step(): return out[1:].reshape(q.shape)  2.06 us

profile of v2, /device:TPU:0, one launch (start us, length us, event | category | flops | bytes accessed | tf_op | source)
XLA Modules:
  0.0 73.3 jit_solution(17804016904964244853)
XLA Ops:
  0.0 71.2 %attend.1 = bf16[33,2,48,128]{3,2,1,0:T(8,128)(2,1)} custom-call(bf16[32,96,128]{2,1,0:T(8,128)(2,1)} %q_ref.1, bf16[32,8192,128]{2,1,0:T(8,128)(2,1)} %bitcast.k_hbm, bf16[32,8192,128]{2,1,0:T(8,128)(2,1)} %bitcast.1.v_hbm), custom_call_target="tpu_custom_call" | custom-call | tf_op jit(solution)/shard_map/attend/pallas_call | solution.py:329
  71.2 2.1 %slice.3 = bf16[32,2,48,128]{3,2,1,0:T(8,128)(2,1)} slice(bf16[33,2,48,128]{3,2,1,0:T(8,128)(2,1)} %attend.1), slice={[1:33], [0:2], [0:48], [0:128]} | slice | bytes 1572864 | tf_op jit(solution)/shard_map/slice | solution.py:361
